TPU v7x, 8 devices: a whole 2x2x1 slice. The times are simulated.
8 devices in a mesh: cz: 2 (over z, y), cy: 2 (over x), cx: 2 (over core).
Axes of the slice: x: 2, y: 2, z: 1, core: 2. Of those that a mesh axis runs over, the one named last changes fastest.
Arguments:
- x: bfloat16 [512, 2048], P(('cx', 'cz'), 'cy')
- w1: bfloat16 [2048, 8192], P('cy', ('cz', 'cx'))
- w2: bfloat16 [8192, 2048], P('cz', ('cy', 'cx'))
Outputs:
- output: bfloat16 [512, 2048], P(('cx', 'cz'), 'cy')
All inputs are finite; a program needn't handle non-finite values.
Results may differ from a plain program's by a relative error of at most 0.0114559.
Values are sent between devices in bfloat16 or wider.
A program may use at most 1 GiB of HBM per device.

v0:
```python
import jax
import jax.numpy as jnp
from jax import lax
from jax.sharding import PartitionSpec as P


def solution(mesh):
    def body(x, w1, w2):
        xg = lax.all_gather(x, "cz", axis=0, tiled=True)
        w1g = lax.all_gather(w1, "cx", axis=1, tiled=True)
        cp = jnp.dot(xg, w1g, preferred_element_type=jnp.float32)
        c = lax.psum_scatter(cp, "cy", scatter_dimension=0, tiled=True).astype(jnp.bfloat16)
        h = jax.nn.gelu(c.astype(jnp.float32), approximate=True).astype(jnp.bfloat16)
        hg = lax.all_gather(h, "cy", axis=0, tiled=True)
        w2g = lax.all_gather(w2, "cx", axis=1, tiled=True)
        zp = jnp.dot(hg, w2g, preferred_element_type=jnp.float32)
        return lax.psum_scatter(zp, "cz", scatter_dimension=0, tiled=True).astype(jnp.bfloat16)

    return jax.shard_map(
        body,
        mesh=mesh,
        in_specs=(P(("cx", "cz"), "cy"), P("cy", ("cz", "cx")), P("cz", ("cy", "cx"))),
        out_specs=P(("cx", "cz"), "cy"),
        check_vma=False,
    )
```

profile of v0, /device:TPU:1, one launch (start us, length us, event | category | flops | bytes accessed | tf_op | source)
XLA Modules:
  0.0 173.2 jit_solution(9877802752243696767)
XLA Ops:
  6.5 0.0 all-gather.4.cloned.1.call-start
  6.5 0.0 copy-start
  6.5 0.7 all-gather.4.cloned.1.call-update
  7.3 0.0 reduce-scatter.3.cloned.1.call-start
  7.3 0.2 copy-done
  7.5 8.7 %all_gather.12 = bf16[256,1024]{1,0:T(8,128)(2,1)S(1)} all-gather(bf16[128,1024]{1,0:T(8,128)(2,1)S(1)} %copy-done), channel_id=1, replica_groups=mesh['cz'=2,'cy'=2,'cx'=2] {'cz'}, dimensions={0}, use_global_device_ids=true | all-gather | bytes 786432 | tf_op jit(solution)/shard_map/all_gather | solution.py:9
  16.2 11.9 %all-gather.4.cloned.1.call-done = bf16[1024,4096]{1,0:T(8,128)(2,1)} async-done(((bf16[1024,2048]{1,0:T(8,128)(2,1)}), bf16[1024,4096]{1,0:T(8,128)(2,1)}) %all-gather.4.cloned.1.call-update) | async-done | bytes 8388624 | tf_op jit(solution)/shard_map/all_gather | solution.py:10
  28.1 7.7 %fusion.6 = f32[256,4096]{1,0:T(8,128)} fusion(bf16[256,1024]{1,0:T(8,128)(2,1)S(1)} %all_gather.12, bf16[1024,4096]{1,0:T(8,128)(2,1)} %all-gather.4.cloned.1.call-done), kind=kOutput, calls=%fused_computation.10 | convolution fusion | flops 2147483648 | bytes 13107200 | tf_op jit(solution)/shard_map/dot_general | solution.py:11
  35.8 0.0 reduce-scatter.3.cloned.1.call-update
  35.8 0.0 all-gather.8.cloned.1.call-start
  35.9 0.7 all-gather.8.cloned.1.call-update
  36.6 0.0 all-gather.6.cloned.1.call-start
  36.6 51.6 %reduce-scatter.3.cloned.1.call-done = f32[128,4096]{1,0:T(8,128)} async-done(((f32[256,4096]{1,0:T(8,128)}), f32[128,4096]{1,0:T(8,128)}) %reduce-scatter.3.cloned.1.call-update) | async-done | bytes 2097168 | tf_op jit(solution)/shard_map/reduce_scatter | solution.py:12
  88.2 3.2 %fusion.5 = bf16[128,4096]{1,0:T(8,128)(2,1)} fusion(f32[128,4096]{1,0:T(8,128)} %reduce-scatter.3.cloned.1.call-done), kind=kLoop, calls=%fused_computation.9 | loop fusion | flops 5767168 | bytes 3145728 | tf_op jit(solution)/shard_map/convert_element_type | solution.py:13
  91.4 0.0 all-gather.6.cloned.1.call-update
  91.5 0.0 reduce-scatter.5.cloned.1.call-start
  91.5 15.9 %all-gather.8.cloned.1.call-done = bf16[4096,1024]{1,0:T(8,128)(2,1)} async-done(((bf16[4096,512]{1,0:T(8,128)(2,1)}), bf16[4096,1024]{1,0:T(8,128)(2,1)}) %all-gather.8.cloned.1.call-update) | async-done | bytes 8388624 | tf_op jit(solution)/shard_map/all_gather | solution.py:15
  107.4 32.3 %all-gather.6.cloned.1.call-done = bf16[256,4096]{1,0:T(8,128)(2,1)} async-done(((bf16[128,4096]{1,0:T(8,128)(2,1)}), bf16[256,4096]{1,0:T(8,128)(2,1)}) %all-gather.6.cloned.1.call-update) | async-done | bytes 2097168 | tf_op jit(solution)/shard_map/all_gather | solution.py:14
  139.7 7.3 %fusion.7 = f32[256,1024]{1,0:T(8,128)} fusion(bf16[256,4096]{1,0:T(8,128)(2,1)} %all-gather.6.cloned.1.call-done, bf16[4096,1024]{1,0:T(8,128)(2,1)} %all-gather.8.cloned.1.call-done), kind=kOutput, calls=%fused_computation.11 | convolution fusion | flops 2147483648 | bytes 11534336 | tf_op jit(solution)/shard_map/dot_general | solution.py:16
  147.1 0.0 reduce-scatter.5.cloned.1.call-update
  147.1 17.8 %reduce-scatter.5.cloned.1.call-done = f32[128,1024]{1,0:T(8,128)} async-done(((f32[256,1024]{1,0:T(8,128)}), f32[128,1024]{1,0:T(8,128)}) %reduce-scatter.5.cloned.1.call-update) | async-done | bytes 524304 | tf_op jit(solution)/shard_map/reduce_scatter | solution.py:17
  164.9 1.8 %convert_element_type.15 = bf16[128,1024]{1,0:T(8,128)(2,1)} convert(f32[128,1024]{1,0:T(8,128)} %reduce-scatter.5.cloned.1.call-done) | non-fusion elementwise | flops 131072 | bytes 786432 | tf_op jit(solution)/shard_map/convert_element_type | solution.py:17
Async XLA Ops:
  6.5 21.6 %all-gather.4.cloned.1.call-start = ((), (), s32[]{:S(2)}) async-start(), calls=%async_computation.2 | async-start | bytes 12582912 | tf_op jit(solution)/shard_map/all_gather | solution.py:10
  6.5 0.9 copy-start
  7.3 81.0 %reduce-scatter.3.cloned.1.call-start = ((), (), s32[]{:S(2)}) async-start(), calls=%async_computation.3 | async-start | bytes 6291456 | tf_op jit(solution)/shard_map/reduce_scatter | solution.py:12
  35.8 71.6 %all-gather.8.cloned.1.call-start = ((), (), s32[]{:S(2)}) async-start(), calls=%async_computation.5 | async-start | bytes 12582912 | tf_op jit(solution)/shard_map/all_gather | solution.py:15
  36.6 103.2 %all-gather.6.cloned.1.call-start = ((), (), s32[]{:S(2)}) async-start(), calls=%async_computation.4 | async-start | bytes 3145728 | tf_op jit(solution)/shard_map/all_gather | solution.py:14
  91.5 73.4 %reduce-scatter.5.cloned.1.call-start = ((), (), s32[]{:S(2)}) async-start(), calls=%async_computation.6 | async-start | bytes 1572864 | tf_op jit(solution)/shard_map/reduce_scatter | solution.py:17
Sparse Core Ops, SparseCore 0:
  8.8 19.2 all-gather.3
  36.0 52.2 reduce-scatter.2
  89.7 17.6 all-gather.7
  108.8 30.9 all-gather.5
  147.2 17.5 reduce-scatter.4
where the time goes:
time: 175 us; the launch traced here: 173 us
  waiting for transfers between devices  131 us (75%)
  matrix products  15 us (9%)
  between operations  13.1 us (7%)
  blocking collectives  8.72 us (5%)
  other arithmetic  5 us (3%)
    reduce_scatter x1, waiting for transfers between devices, body(): lax.psum_scatter(cp, 'cy', scatter_dimension=0, tiled=True)  51.6 us
    all_gather x1, waiting for transfers between devices, body(): hg = lax.all_gather(h, 'cy', axis=0, tiled=True)  32.3 us
    reduce_scatter x1, waiting for transfers between devices, body(): lax.psum_scatter(zp, 'cz', scatter_dimension=0, tiled=True)  17.8 us
    all_gather x1, waiting for transfers between devices, body(): w2g = lax.all_gather(w2, 'cx', axis=1, tiled=True)  15.9 us
    all_gather x1, waiting for transfers between devices, body(): w1g = lax.all_gather(w1, 'cx', axis=1, tiled=True)  11.9 us
    all_gather x1, blocking collectives, body(): xg = lax.all_gather(x, 'cz', axis=0, tiled=True)  8.72 us
    dot_general x1, matrix products, body(): cp = jnp.dot(xg, w1g, preferred_element_type=jnp.float32)  7.68 us
    dot_general x1, matrix products, body(): zp = jnp.dot(hg, w2g, preferred_element_type=jnp.float32)  7.34 us
  transfers between devices with their start and end apart: 5, of which 5 were waited for; matrix products, arithmetic and copies ran while one was open for 2% of the time, Pallas kernels for 0%

commit v1 on v0

v1 whole, which is shorter than its diff:
```python
import functools

import jax
import jax.numpy as jnp
from jax import lax
from jax.experimental import pallas as pl
from jax.experimental.pallas import tpu as pltpu
from jax.sharding import PartitionSpec as P

MESH = pl.DeviceIdType.MESH
F32 = jnp.float32
BF16 = jnp.bfloat16
G = 64


def gelu(c):
    c = c.astype(F32)
    return 0.5 * c * (1.0 + jnp.tanh(0.7978845608028654 * (c + 0.044715 * (c * c * c))))


def kernel(x_ref, w1_ref, w2_ref, out_ref,
           xs, w1s, w1o, w2s, psend, precv, pown, h, zp, zr,
           lsem, xss, xrs, pss, prs, hss, hrs, dss, drs, fss, frs, zss, zrs):
    cz, cy, cx = (lax.axis_index(a) for a in ("cz", "cy", "cx"))
    oz, oy, ox = 1 - cz, 1 - cy, 1 - cx
    dev_x = (cz, oy, cx)
    dev_c = (cz, cy, ox)
    dev_y = (oz, cy, cx)
    dev_d = (oz, cy, ox)

    rows, depth = x_ref.shape
    q = rows // G
    n = 4 * q
    half = w1_ref.shape[1] // 2
    wide = w2_ref.shape[1]

    def own_pair(i):
        return i if i < q // 2 else i + q

    def rcopy(src, dst, ss, rs, dev):
        return pltpu.make_async_remote_copy(src_ref=src, dst_ref=dst, send_sem=ss, recv_sem=rs, device_id=dev,
                                            device_id_type=MESH)

    loads_x = [pltpu.make_async_copy(x_ref.at[pl.ds(i * G, G)], xs.at[2 * own_pair(i)], lsem.at[i]) for i in range(q)]
    load_s = pltpu.make_async_copy(w1_ref.at[:, pl.ds(pl.multiple_of(oy * half, half), half)], w1s, lsem.at[q])
    load_o = pltpu.make_async_copy(w1_ref.at[:, pl.ds(pl.multiple_of(cy * half, half), half)], w1o, lsem.at[q + 1])
    loads_2 = []
    for j, (a, b) in enumerate(((cx, cy), (cx, oy), (ox, cy), (ox, oy))):
        loads_2.append(pltpu.make_async_copy(w2_ref.at[pl.ds(pl.multiple_of((2 * a + b) * half, half), half)], w2s.at[j],
                                             lsem.at[q + 2 + j]))
    for c in loads_x + [load_s, load_o] + loads_2:
        c.start()

    barrier = pltpu.get_barrier_semaphore()
    for dev in (dev_x, dev_c, dev_y, dev_d):
        pl.semaphore_signal(barrier, inc=1, device_id=dev, device_id_type=MESH)
    for c in loads_x:
        c.wait()
    pl.semaphore_wait(barrier, 4)

    x_sends = []
    for i in range(q):
        src = xs.at[2 * own_pair(i)]
        for d, (dev, u) in enumerate(((dev_c, 2 * own_pair(i) + 1), (dev_y, 2 * (i + q // 2)), (dev_d, 2 * (i + q // 2) + 1))):
            c = rcopy(src, xs.at[u], xss.at[d, i], xrs.at[u], dev)
            c.start()
            x_sends.append(c)
    load_s.wait()

    def p_copy(u):
        return rcopy(psend.at[u], precv.at[u], pss.at[u], prs.at[u], dev_x)

    def h_copy(u):
        return rcopy(h.at[0, u], h.at[1, u], hss.at[u], hrs.at[u], dev_x)

    def d_copy(u):
        return rcopy(h.at[0, u], h.at[2, u + 1 - 2 * lax.rem(u, 2)], dss.at[u], drs.at[u + 1 - 2 * lax.rem(u, 2)], dev_c)

    def d_wait(u):
        rcopy(h.at[0, u], h.at[2, u], dss.at[u], drs.at[u], dev_c).wait_recv()

    def f_copy(u):
        return rcopy(h.at[1, u], h.at[3, u + 1 - 2 * lax.rem(u, 2)], fss.at[u], frs.at[u + 1 - 2 * lax.rem(u, 2)], dev_c)

    def f_wait(u):
        rcopy(h.at[1, u], h.at[3, u], fss.at[u], frs.at[u], dev_c).wait_recv()

    def partial(u):
        psend[u] = jnp.dot(xs[u], w1s[...], preferred_element_type=F32)
        p_copy(u).start()

    def stay(u):
        pown[u] = jnp.dot(xs[u], w1o[...], preferred_element_type=F32)

    def x_wait(u):
        rcopy(xs.at[u], xs.at[u], xss.at[0, 0], xrs.at[u], dev_c).wait_recv()

    partial(0)
    load_o.wait()
    stay(0)

    def layer1(u, carry):
        i = lax.rem(u, 2)
        mine = jnp.logical_and(i == 0, jnp.logical_or(u < q, u >= 3 * q))

        @pl.when(jnp.logical_not(mine))
        def _():
            x_wait(u)

        partial(u)
        stay(u)
        return carry

    lax.fori_loop(1, n, layer1, 0)

    def activate(u, carry):
        p_copy(u).wait_recv()
        c = (pown[u] + precv[u]).astype(BF16)
        h[0, u] = gelu(c).astype(BF16)
        h_copy(u).start()
        d_copy(u).start()
        return carry

    lax.fori_loop(0, n, activate, 0)
    for c in loads_2:
        c.wait()

    def forward(u):
        h_copy(u).wait_recv()
        f_copy(u).start()

    def z_dev(u):
        i, k = lax.rem(u, 2), u // 2
        other = jnp.logical_and(k >= q // 2, k < q // 2 + q).astype(jnp.int32)
        late = (k >= q // 2 + q).astype(jnp.int32)
        sub = k - other * (q // 2) - late * q
        dev = (cz + other - 2 * other * cz, cy, cx + i - 2 * i * cx)
        slot = other * (1 + i)
        return dev, slot, sub

    def z_copy(u):
        dev, slot, sub = z_dev(u)
        return rcopy(zp.at[u], zr.at[slot, sub], zss.at[u], zrs.at[slot, sub], dev)

    def kept(u):
        return jnp.logical_and(lax.rem(u, 2) == 0, jnp.logical_or(u < q, u >= 3 * q))

    def second(u):
        acc = jnp.dot(h[0, u], w2s[0], preferred_element_type=F32)
        d_wait(u)
        acc += jnp.dot(h[2, u], w2s[2], preferred_element_type=F32)
        acc += jnp.dot(h[1, u], w2s[1], preferred_element_type=F32)
        f_wait(u)
        acc += jnp.dot(h[3, u], w2s[3], preferred_element_type=F32)
        zp[u] = acc

        @pl.when(jnp.logical_not(kept(u)))
        def _():
            z_copy(u).start()

    forward(0)
    forward(1)

    def layer2(u, carry):
        forward(u + 2)
        second(u)
        return carry

    lax.fori_loop(0, n - 2, layer2, 0)
    second(jnp.int32(n - 2))
    second(jnp.int32(n - 1))

    left = pl.multiple_of(cx * wide, wide)
    right = pl.multiple_of(ox * wide, wide)
    for i in range(q):
        for slot in range(3):
            rcopy(zp.at[0], zr.at[slot, i], zss.at[0], zrs.at[slot, i], dev_c).wait_recv()
        out_ref[pl.ds(i * G, G), pl.ds(left, wide)] = (zp[2 * own_pair(i)] + zr[1, i]).astype(BF16)
        out_ref[pl.ds(i * G, G), pl.ds(right, wide)] = (zr[0, i] + zr[2, i]).astype(BF16)

    for c in x_sends:
        c.wait_send()

    def finish(u, carry):
        p_copy(u).wait_send()
        h_copy(u).wait_send()
        d_copy(u).wait_send()
        f_copy(u).wait_send()

        @pl.when(jnp.logical_not(kept(u)))
        def _():
            z_copy(u).wait_send()

        return carry

    lax.fori_loop(0, n, finish, 0)


def solution(mesh):
    def body(x, w1, w2):
        rows, depth = x.shape
        q = rows // G
        n = 4 * q
        half = w1.shape[1] // 2
        wide = w2.shape[1]
        dma = pltpu.SemaphoreType.DMA
        anywhere = pl.BlockSpec(memory_space=pl.ANY)
        return pl.pallas_call(
            kernel,
            out_shape=jax.ShapeDtypeStruct((rows, 2 * wide), BF16),
            in_specs=[anywhere] * 3,
            out_specs=pl.BlockSpec(memory_space=pltpu.VMEM),
            scratch_shapes=[
                pltpu.VMEM((n, G, depth), BF16),
                pltpu.VMEM((depth, half), BF16),
                pltpu.VMEM((depth, half), BF16),
                pltpu.VMEM((4, half, wide), BF16),
                pltpu.VMEM((n, G, half), F32),
                pltpu.VMEM((n, G, half), F32),
                pltpu.VMEM((n, G, half), F32),
                pltpu.VMEM((4, n, G, half), BF16),
                pltpu.VMEM((n, G, wide), F32),
                pltpu.VMEM((3, q, G, wide), F32),
                dma((q + 6,)),
                dma((3, q)), dma((n,)),
                dma((n,)), dma((n,)),
                dma((n,)), dma((n,)),
                dma((n,)), dma((n,)),
                dma((n,)), dma((n,)),
                dma((n,)), dma((3, q)),
            ],
            compiler_params=pltpu.CompilerParams(
                collective_id=0, has_side_effects=True, vmem_limit_bytes=60 * 1024 * 1024,
            ),
            cost_estimate=pl.CostEstimate(flops=4 * 512 * 1024 * 2048 * 2, bytes_accessed=9 << 20, transcendentals=512 * 1024),
        )(x, w1, w2)

    return jax.shard_map(
        body,
        mesh=mesh,
        in_specs=(P(("cx", "cz"), "cy"), P("cy", ("cz", "cx")), P("cz", ("cy", "cx"))),
        out_specs=P(("cx", "cz"), "cy"),
        check_vma=False,
    )
```

time: 175 us -> 82.5 us (0.47)
  waiting for transfers between devices: 131 us -> 0 us
  Pallas kernels: 0 us -> 80.6 us
  matrix products: 15 us -> 0 us
  between operations: 13.1 us -> 0.01 us
  blocking collectives: 8.72 us -> 0 us
  other arithmetic: 5 us -> 0 us
    pallas_call x0 -> x1, Pallas kernels: none -> 80.6 us  [body(): pl.pallas_call(kernel, out_shape=jax.ShapeDtypeStruct((rows, 2 * wide), B...]
    reduce_scatter x2 -> x0, waiting for transfers between devices: 69.4 us -> none  [the longest x1 51.6 us: body(): lax.psum_scatter(cp, 'cy', scatter_dimension=0, tiled=True)]
    all_gather x3 -> x0, waiting for transfers between devices: 60.1 us -> none  [the longest x1 32.3 us: body(): hg = lax.all_gather(h, 'cy', axis=0, tiled=True)]
    dot_general x2 -> x0, matrix products: 15 us -> none  [the longest x1 7.68 us: body(): cp = jnp.dot(xg, w1g, preferred_element_type=jnp.float32)]
    all_gather x1 -> x0, blocking collectives: 8.72 us -> none  [body(): xg = lax.all_gather(x, 'cz', axis=0, tiled=True)]
    convert_element_type x2 -> x0, other arithmetic: 5 us -> none  [the longest x1 3.23 us: body(): jax.nn.gelu(c.astype(jnp.float32), approximate=True).astype(jnp.bfloat16)]
  transfers between devices with their start and end apart: 5 -> 0, of which waited for: 5 -> 0; matrix products, arithmetic and copies ran while one was open for 2% -> 0% of each run, Pallas kernels for 0% -> 0%
where the time goes in v1:
time: 82.5 us; the launch traced here: 82.3 us
  Pallas kernels  80.6 us (98%)
  local copies, waits for them, and re-layouts  1.67 us (2%)
    pallas_call x1, Pallas kernels, body(): pl.pallas_call(kernel, out_shape=jax.ShapeDtypeStruct((rows, 2 * wide), B...  80.6 us
    unnamed x1, local copies, waits for them, and re-layouts  1.67 us

profile of v1, /device:TPU:1, one launch (start us, length us, event | category | flops | bytes accessed | tf_op | source)
XLA Modules:
  0.0 82.3 jit_solution(6400143631242831431)
XLA Ops:
  0.0 80.6 %shard_map.37 = bf16[128,1024]{1,0:T(8,128)(2,1)} custom-call(bf16[128,1024]{1,0:T(8,128)(2,1)} %x_ref.1, bf16[1024,2048]{1,0:T(8,128)(2,1)} %w1_ref.1, bf16[4096,512]{1,0:T(8,128)(2,1)} %w2_ref.1), custom_call_target="tpu_custom_call" | custom-call | flops 8589934592 | bytes 9437184 | tf_op jit(solution)/shard_map/pallas_call | solution.py:208
  80.6 1.7 %copy.5 = bf16[128,1024]{1,0:T(8,128)(2,1)} copy(bf16[128,1024]{1,0:T(8,128)(2,1)} %shard_map.37) | data formatting | bytes 524288

commit v2 on v1

v2 whole, which is shorter than its diff:
```python
import functools

import jax
import jax.numpy as jnp
from jax import lax
from jax.experimental import pallas as pl
from jax.experimental.pallas import tpu as pltpu
from jax.sharding import PartitionSpec as P

MESH = pl.DeviceIdType.MESH
F32 = jnp.float32
BF16 = jnp.bfloat16
G = 64
LAG = 1
PIECES = 4


def gelu(c):
    c = c.astype(F32)
    return 0.5 * c * (1.0 + jnp.tanh(0.7978845608028654 * (c + 0.044715 * (c * c * c))))


def dot(a, b):
    return jnp.dot(a, b, preferred_element_type=F32)


def kernel(x_ref, w1_ref, w2_ref, out_ref,
           xs, w1s, w1o, w2s, psend, precv, pown, h, zp, zr,
           lsem, xss, xrs, wss, wrs, pss, prs, hss, hrs, zss, zrs):
    cz, cy, cx = (lax.axis_index(a) for a in ("cz", "cy", "cx"))
    oz, oy, ox = 1 - cz, 1 - cy, 1 - cx
    dev_x = (cz, oy, cx)
    dev_c = (cz, cy, ox)
    dev_y = (oz, cy, cx)
    dev_d = (oz, cy, ox)

    rows = x_ref.shape[0]
    q = rows // G
    n = 4 * q
    e = q // 2
    half = w1_ref.shape[1] // 2
    wide = w2_ref.shape[1]
    piece = half // PIECES

    def own_unit(i):
        return 2 * i if i < e else 2 * (i + q) + 1

    def partner_unit(i):
        return 2 * i + 1 if i < e else 2 * (i + q)

    def rcopy(src, dst, ss, rs, dev):
        return pltpu.make_async_remote_copy(src_ref=src, dst_ref=dst, send_sem=ss, recv_sem=rs, device_id=dev,
                                            device_id_type=MESH)

    def block(i, size):
        return pl.ds(pl.multiple_of(i * size, size), size)

    loads_x = [pltpu.make_async_copy(x_ref.at[pl.ds(i * G, G)], xs.at[own_unit(i)], lsem.at[i]) for i in range(q)]
    loads_s = [pltpu.make_async_copy(w1_ref.at[:, pl.ds(pl.multiple_of(oy * half + i * piece, piece), piece)],
                                     w1s.at[:, pl.ds(i * piece, piece)], lsem.at[q + i]) for i in range(PIECES)]
    load_o = pltpu.make_async_copy(w1_ref.at[:, block(cy, half)], w1o, lsem.at[q + PIECES])
    loads_2 = [pltpu.make_async_copy(w2_ref.at[block(2 * cx + b, half)], w2s.at[j, :, block(cx, wide)],
                                     lsem.at[q + PIECES + 1 + j]) for j, b in enumerate((cy, oy))]
    sends_2 = [rcopy(w2_ref.at[block(2 * ox + b, half)], w2s.at[j, :, block(cx, wide)], wss.at[j], wrs.at[j], dev_c)
               for j, b in enumerate((cy, oy))]
    for c in loads_x[:1] + loads_s[:1] + loads_x[1:] + loads_s[1:]:
        c.start()

    barrier = pltpu.get_barrier_semaphore()
    for dev in (dev_x, dev_c, dev_y, dev_d):
        pl.semaphore_signal(barrier, inc=1, device_id=dev, device_id_type=MESH)

    def first(i):
        cols = pl.ds(i * piece, piece)
        loads_s[i].wait()
        psend[0, :, cols] = dot(xs[0], w1s[:, cols])

    def first_send(i):
        cols = pl.ds(i * piece, piece)
        rcopy(psend.at[0, :, cols], precv.at[0, :, cols], pss.at[0], prs.at[0], dev_x).start()

    loads_x[0].wait()
    first(0)
    pl.semaphore_wait(barrier, 4)
    first_send(0)

    x_sends = []

    def send_x(i, dev, slot, u):
        c = rcopy(xs.at[own_unit(i)], xs.at[u], xss.at[slot, i], xrs.at[u], dev)
        c.start()
        x_sends.append(c)

    for i in range(q):
        if i:
            loads_x[i].wait()
        send_x(i, dev_c, 0, partner_unit(i))
        send_x(i, dev_y, 1, 2 * (i + e))
        send_x(i, dev_d, 2, 2 * (i + e) + 1)
    for i in range(1, PIECES):
        first(i)
        first_send(i)
    load_o.start()
    for c in sends_2 + loads_2:
        c.start()

    def p_copy(u):
        return rcopy(psend.at[u], precv.at[u], pss.at[u], prs.at[u], dev_x)

    def h_copy(u):
        return rcopy(h.at[0, u], h.at[1, u], hss.at[u], hrs.at[u], dev_x)

    def partial(u):
        psend[u] = dot(xs[u], w1s[...])
        p_copy(u).start()

    def stay(u):
        pown[u] = dot(xs[u], w1o[...])

    def x_wait(u):
        rcopy(xs.at[u], xs.at[u], xss.at[0, 0], xrs.at[u], dev_c).wait_recv()

    def own(u):
        i = lax.rem(u, 2)
        return jnp.logical_or(jnp.logical_and(i == 0, u < q), jnp.logical_and(i == 1, u >= 3 * q))

    def layer1(u):
        @pl.when(jnp.logical_not(own(u)))
        def _():
            x_wait(u)

        partial(u)
        stay(u)

    def activate(u):
        p_copy(u).wait_recv()
        c = (pown[u] + precv[u]).astype(BF16)
        h[0, u] = gelu(c).astype(BF16)
        h_copy(u).start()

    def z_copy(u):
        i, k = lax.rem(u, 2), u // 2
        other = jnp.logical_and(k >= e, k < e + q).astype(jnp.int32)
        late = (k >= e + q).astype(jnp.int32)
        sub = k - other * e - late * q
        swap = jnp.where(late == 1, 1 - i, i)
        dev = (cz + other - 2 * other * cz, cy, cx + swap - 2 * swap * cx)
        slot = other * (1 + swap)
        return rcopy(zp.at[u], zr.at[slot, sub], zss.at[u], zrs.at[slot, sub], dev)

    def layer2(u):
        zp[u] = dot(h[0, u], w2s[0])
        h_copy(u).wait_recv()
        zp[u] += dot(h[1, u], w2s[1])

        @pl.when(jnp.logical_not(own(u)))
        def _():
            z_copy(u).start()

    load_o.wait()
    stay(0)

    def loop(lo, hi, *stages):
        def step(u, carry):
            for stage, shift in stages:
                stage(u + shift)
            return carry

        lax.fori_loop(lo, hi, step, 0)

    loop(1, LAG + 1, (layer1, 0))
    loop(0, LAG, (activate, 0), (layer1, LAG + 1))
    for c in loads_2:
        c.wait()
    for j, b in enumerate((cy, oy)):
        rcopy(w2_ref.at[block(2 * ox + b, half)], w2s.at[j, :, block(ox, wide)], wss.at[j], wrs.at[j], dev_c).wait_recv()
    loop(LAG, n - LAG - 1, (activate, 0), (layer1, LAG + 1), (layer2, -LAG))
    loop(n - LAG - 1, n, (activate, 0), (layer2, -LAG))
    loop(n - LAG, n - 1, (layer2, 0))

    def arrived(i):
        for slot in range(3):
            rcopy(zp.at[0], zr.at[slot, i], zss.at[0], zrs.at[slot, i], dev_c).wait_recv()
        return zr[0, i] + zr[1, i] + zr[2, i]

    for i in range(q - 1):
        out_ref[pl.ds(i * G, G)] = (zp[own_unit(i)] + arrived(i)).astype(BF16)
    zp[n - 1] = dot(h[0, n - 1], w2s[0]) + arrived(q - 1)
    h_copy(n - 1).wait_recv()
    out_ref[pl.ds((q - 1) * G, G)] = (zp[n - 1] + dot(h[1, n - 1], w2s[1])).astype(BF16)

    for c in x_sends + sends_2:
        c.wait_send()

    def finish(u):
        p_copy(u).wait_send()
        h_copy(u).wait_send()

        @pl.when(jnp.logical_not(own(u)))
        def _():
            z_copy(u).wait_send()

    loop(0, n, (finish, 0))


def solution(mesh):
    def body(x, w1, w2):
        rows, depth = x.shape
        q = rows // G
        n = 4 * q
        half = w1.shape[1] // 2
        wide = w2.shape[1]
        dma = pltpu.SemaphoreType.DMA
        anywhere = pl.BlockSpec(memory_space=pl.ANY)
        return pl.pallas_call(
            kernel,
            out_shape=jax.ShapeDtypeStruct((rows, 2 * wide), BF16),
            in_specs=[anywhere] * 3,
            out_specs=pl.BlockSpec(memory_space=pltpu.VMEM),
            scratch_shapes=[
                pltpu.VMEM((n, G, depth), BF16),
                pltpu.VMEM((depth, half), BF16),
                pltpu.VMEM((depth, half), BF16),
                pltpu.VMEM((2, half, 2 * wide), BF16),
                pltpu.VMEM((n, G, half), F32),
                pltpu.VMEM((n, G, half), F32),
                pltpu.VMEM((n, G, half), F32),
                pltpu.VMEM((2, n, G, half), BF16),
                pltpu.VMEM((n, G, 2 * wide), F32),
                pltpu.VMEM((3, q, G, 2 * wide), F32),
                dma((q + PIECES + 3,)),
                dma((3, q)), dma((n,)),
                dma((2,)), dma((2,)),
                dma((n,)), dma((n,)),
                dma((n,)), dma((n,)),
                dma((n,)), dma((3, q)),
            ],
            compiler_params=pltpu.CompilerParams(
                collective_id=0, has_side_effects=True, vmem_limit_bytes=60 * 1024 * 1024,
            ),
            cost_estimate=pl.CostEstimate(flops=4 * 512 * 1024 * 2048 * 2, bytes_accessed=9 << 20, transcendentals=512 * 1024),
        )(x, w1, w2)

    return jax.shard_map(
        body,
        mesh=mesh,
        in_specs=(P(("cx", "cz"), "cy"), P("cy", ("cz", "cx")), P("cz", ("cy", "cx"))),
        out_specs=P(("cx", "cz"), "cy"),
        check_vma=False,
    )
```

time: 82.5 us -> 77 us (0.933)
  Pallas kernels: 80.6 us -> 74.6 us
    pallas_call x1, Pallas kernels: 80.6 us -> 74.6 us  [body(): pl.pallas_call(kernel, out_shape=jax.ShapeDtypeStruct((rows, 2 * wide), B...]
where the time goes in v2:
time: 77 us; the launch traced here: 76.3 us
  Pallas kernels  74.6 us (97%)
  local copies, waits for them, and re-layouts  1.67 us (2%)
    pallas_call x1, Pallas kernels, body(): pl.pallas_call(kernel, out_shape=jax.ShapeDtypeStruct((rows, 2 * wide), B...  74.6 us
    unnamed x1, local copies, waits for them, and re-layouts  1.67 us

profile of v2, /device:TPU:1, one launch (start us, length us, event | category | flops | bytes accessed | tf_op | source)
XLA Modules:
  0.0 76.3 jit_solution(17774361136657789372)
XLA Ops:
  0.0 74.6 %shard_map.37 = bf16[128,1024]{1,0:T(8,128)(2,1)} custom-call(bf16[128,1024]{1,0:T(8,128)(2,1)} %x_ref.1, bf16[1024,2048]{1,0:T(8,128)(2,1)} %w1_ref.1, bf16[4096,512]{1,0:T(8,128)(2,1)} %w2_ref.1), custom_call_target="tpu_custom_call" | custom-call | flops 8589934592 | bytes 9437184 | tf_op jit(solution)/shard_map/pallas_call | solution.py:215
  74.6 1.7 %copy.5 = bf16[128,1024]{1,0:T(8,128)(2,1)} copy(bf16[128,1024]{1,0:T(8,128)(2,1)} %shard_map.37) | data formatting | bytes 524288
